TPU v7x, 32 devices: a whole 2x2x4 slice. The times are simulated.
32 devices in a mesh: dp: 8 (over z, core), tp: 4 (over y, x).
Axes of the slice: x: 2, y: 2, z: 4, core: 2. Of those that a mesh axis runs over, the one named last changes fastest.
Arguments:
- master: float32 [4096, 10240], P(('dp', 'tp')), may hold values from -0.09375 to 0.09375
- grad: float32 [4096, 10240], P(('dp', 'tp')), may hold values from -0.006 to 0.006
- exp_avg: float32 [4096, 10240], P(('dp', 'tp')), may hold values from -0.006 to 0.006
- exp_avg_sq: float32 [4096, 10240], P(('dp', 'tp')), may hold values from 1e-08 to 1e-05
Outputs:
- new_master: float32 [4096, 10240], P(('dp', 'tp'))
- new_avg: float32 [4096, 10240], P(('dp', 'tp'))
- new_avg_sq: float32 [4096, 10240], P(('dp', 'tp'))
- engine_qkv: bfloat16 [4096, 10240], P(None, 'tp')
All inputs are finite; a program needn't handle non-finite values.
Results may differ from a plain program's by a relative error of at most 0.001.
Values may be sent and summed in bfloat16 or wider, within the bound.
A program may use at most 128 MiB of HBM per device.

v0:
```python
import jax
import jax.numpy as jnp
from jax import lax
from jax.sharding import PartitionSpec as P

QH = 64
KVH = 8
HS = 128


def joined_slices(weights, tp_count):
    rows = weights.shape[0]
    query = weights[:, : QH * HS].reshape(rows, tp_count, QH // tp_count * HS)
    keys = weights[:, QH * HS : (QH + KVH) * HS].reshape(rows, tp_count, KVH // tp_count * HS)
    values = weights[:, (QH + KVH) * HS :].reshape(rows, tp_count, KVH // tp_count * HS)
    return jnp.concatenate([query, keys, values], axis=2).reshape(rows, -1)


def body(master, grad, exp_avg, exp_avg_sq):
    corr_one = 1.0 - 0.9**10
    corr_two = 1.0 - 0.999**10
    new_avg = 0.9 * exp_avg + 0.1 * grad
    new_avg_sq = 0.999 * exp_avg_sq + 0.001 * grad * grad
    update = new_avg / corr_one / (jnp.sqrt(new_avg_sq / corr_two) + 1e-08)
    new_master = master - 0.001 * (update + 0.1 * master)
    tp_count = lax.axis_size("tp")
    ordered = joined_slices(new_master, tp_count).astype(jnp.bfloat16)
    group_rows = lax.all_to_all(ordered, "tp", split_axis=1, concat_axis=0, tiled=True)
    engine_qkv = lax.all_gather(group_rows, "dp", axis=0, tiled=True)
    return (new_master, new_avg, new_avg_sq, engine_qkv)


def solution(mesh):
    in_specs = (
        P(("dp", "tp"), None),
        P(("dp", "tp"), None),
        P(("dp", "tp"), None),
        P(("dp", "tp"), None),
    )
    out_specs = (P(("dp", "tp"), None), P(("dp", "tp"), None), P(("dp", "tp"), None), P(None, "tp"))
    return jax.shard_map(body, mesh=mesh, in_specs=in_specs, out_specs=out_specs, check_vma=False)
```

profile of v0, /device:TPU:0, one launch (start us, length us, event | category | flops | bytes accessed | tf_op | source)
XLA Modules:
  0.0 267.6 jit_solution(15748844206019149272)
XLA Ops:
  7.2 0.0 all-gather.2.cloned.1.call-start
  7.2 14.4 %fusion.1 = (bf16[128,10240]{1,0:T(8,128)(2,1)S(1)}, f32[128,10240]{1,0:T(8,128)}, f32[128,10240]{1,0:T(8,128)}, f32[128,10240]{1,0:T(8,128)}) fusion(f32[128,10240]{1,0:T(8,128)} %param.4, f32[128,10240]{1,0:T(8,128)} %param.5, f32[128,10240]{1,0:T(8,128)} %param.6, f32[128,10240]{1,0:T(8,128)} %param.7), kind=kLoop, calls=%fused_computation.8 | loop fusion | flops 20971520 | bytes 39321600 | tf_op jit(solution)/shard_map/convert.8
  21.6 0.1 slice.15
  21.8 0.1 copy.17
  22.0 0.2 pad_maximum_fusion
  22.2 36.1 %all_to_all.16 = bf16[128,4,2560]{2,0,1:T(8,128)(2,1)} all-to-all(bf16[128,4,2560]{2,0,1:T(8,128)(2,1)S(1)} %pad_maximum_fusion), channel_id=1, replica_groups=mesh['dp'=8,'tp'=4] {'tp'}, dimensions={1} | all-to-all | bytes 5242880 | tf_op jit(solution)/shard_map/all_to_all | solution.py:28
  58.3 0.0 all-gather.2.cloned.1.call-update
  58.3 185.3 %all-gather.2.cloned.1.call-done = bf16[4096,2560]{1,0:T(8,128)(2,1)} async-done(((bf16[512,2560]{1,0:T(8,128)(2,1)}), bf16[4096,2560]{1,0:T(8,128)(2,1)}) %all-gather.2.cloned.1.call-update) | async-done | bytes 20971536 | tf_op jit(solution)/shard_map/all_gather | solution.py:29
  243.6 17.1 %copy.19 = bf16[4096,2560]{1,0:T(8,128)(2,1)} copy(bf16[4096,2560]{1,0:T(8,128)(2,1)} %all-gather.2.cloned.1.call-done) | data formatting | bytes 41943040
  (2 shorter events, 0.1 us)
Async XLA Ops:
  7.2 236.5 %all-gather.2.cloned.1.call-start = ((), (), s32[]{:S(2)}) async-start(), calls=%async_computation.1 | async-start | bytes 23592960 | tf_op jit(solution)/shard_map/all_gather | solution.py:29
Sparse Core Ops, SparseCore 0:
  58.4 185.1 all-gather.1
where the time goes:
time: 268 us
  waiting for transfers between devices  185 us (69%)
  blocking collectives  36.1 us (13%)
  local copies, waits for them, and re-layouts  17.5 us (7%)
  other arithmetic  14.6 us (5%)
  between operations  14.1 us (5%)
    all_gather x1, waiting for transfers between devices, body(): engine_qkv = lax.all_gather(group_rows, 'dp', axis=0, tiled=True)  185 us
    all_to_all x1, blocking collectives, body(): lax.all_to_all(ordered, 'tp', split_axis=1, concat_axis=0, tiled=True)  36.1 us
    unnamed x1, local copies, waits for them, and re-layouts  17.1 us
    another operation x1, other arithmetic  14.4 us
  transfers between devices with their start and end apart: 1, of which 1 were waited for; matrix products, arithmetic and copies ran while one was open for 0% of the time, Pallas kernels for 0%

commit v1 on v0

--- a/solution.py
+++ b/solution.py
@@ -25,7 +25,10 @@
     new_master = master - 0.001 * (update + 0.1 * master)
     tp_count = lax.axis_size("tp")
     ordered = joined_slices(new_master, tp_count).astype(jnp.bfloat16)
-    group_rows = lax.all_to_all(ordered, "tp", split_axis=1, concat_axis=0, tiled=True)
+    group_rows = jnp.concatenate(
+        lax.all_to_all(jnp.stack(jnp.split(ordered, lax.axis_size("tp"), axis=1)), "tp", 0, 0),
+        axis=0,
+    )
     engine_qkv = lax.all_gather(group_rows, "dp", axis=0, tiled=True)
     return (new_master, new_avg, new_avg_sq, engine_qkv)
 

time: 268 us -> 275 us (1.026)
  local copies, waits for them, and re-layouts: 17.5 us -> 23 us
    reshape x1, local copies, waits for them, and re-layouts: 0.14 us -> 3.32 us  [joined_slices(): query = weights[:, :QH * HS].reshape(rows, tp_count, QH // tp_count * HS)]
    unnamed x1 -> x2, local copies, waits for them, and re-layouts: 17.1 us -> 17.6 us
    another operation x1 -> x2, other arithmetic: 14.4 us -> 14.7 us
where the time goes in v1:
time: 275 us
  waiting for transfers between devices  185 us (67%)
  blocking collectives  36.1 us (13%)
  local copies, waits for them, and re-layouts  23 us (8%)
  other arithmetic  16.1 us (6%)
  between operations  14.1 us (5%)
    all_gather x1, waiting for transfers between devices, body(): engine_qkv = lax.all_gather(group_rows, 'dp', axis=0, tiled=True)  185 us
    all_to_all x1, blocking collectives, body(): lax.all_to_all(jnp.stack(jnp.split(ordered, lax.axis_size('tp'), axis=1))...  36.1 us
    unnamed x2, local copies, waits for them, and re-layouts  17.6 us
    another operation x1, other arithmetic  14.4 us
  transfers between devices with their start and end apart: 1, of which 1 were waited for; matrix products, arithmetic and copies ran while one was open for 0% of the time, Pallas kernels for 0%

profile of v1, /device:TPU:0, one launch (start us, length us, event | category | flops | bytes accessed | tf_op | source)
XLA Modules:
  0.0 274.7 jit_solution(9596857814882081816)
XLA Ops:
  7.2 0.0 all-gather.2.cloned.1.call-start
  7.2 14.4 %fusion.1 = (bf16[128,10240]{1,0:T(8,128)(2,1)S(1)}, f32[128,10240]{1,0:T(8,128)}, f32[128,10240]{1,0:T(8,128)}, f32[128,10240]{1,0:T(8,128)}) fusion(f32[128,10240]{1,0:T(8,128)} %param.4, f32[128,10240]{1,0:T(8,128)} %param.5, f32[128,10240]{1,0:T(8,128)} %param.6, f32[128,10240]{1,0:T(8,128)} %param.7), kind=kLoop, calls=%fused_computation.10 | loop fusion | flops 20971520 | bytes 39321600 | tf_op jit(solution)/shard_map/convert.8
  21.6 1.5 slice.15
  23.1 3.3 %reshape.25 = bf16[128,4,2048]{2,1,0:T(4,128)(2,1)S(1)} reshape(bf16[128,8192]{1,0:T(8,128)(2,1)} %slice.15) | data formatting | bytes 4194304 | tf_op jit(solution)/shard_map/reshape | solution.py:13
  26.4 0.2 reshape.26
  26.6 0.2 reshape.27
  26.8 1.4 pad_maximum_fusion
  28.2 0.5 copy.8
  28.7 0.2 slice_bitcast_fusion.3
  28.9 0.3 pad_maximum_fusion.1
  29.2 36.1 %all_to_all.5 = bf16[4,128,2560]{2,1,0:T(8,128)(2,1)} all-to-all(bf16[4,128,2560]{2,1,0:T(8,128)(2,1)S(1)} %pad_maximum_fusion.1), channel_id=1, replica_groups=mesh['dp'=8,'tp'=4] {'tp'}, dimensions={0} | all-to-all | bytes 5242880 | tf_op jit(solution)/shard_map/all_to_all | solution.py:29
  65.3 0.0 all-gather.2.cloned.1.call-update
  65.4 185.3 %all-gather.2.cloned.1.call-done = bf16[4096,2560]{1,0:T(8,128)(2,1)} async-done(((bf16[512,2560]{1,0:T(8,128)(2,1)}), bf16[4096,2560]{1,0:T(8,128)(2,1)}) %all-gather.2.cloned.1.call-update) | async-done | bytes 20971536 | tf_op jit(solution)/shard_map/all_gather | solution.py:32
  250.7 17.1 %copy.10 = bf16[4096,2560]{1,0:T(8,128)(2,1)} copy(bf16[4096,2560]{1,0:T(8,128)(2,1)} %all-gather.2.cloned.1.call-done) | data formatting | bytes 41943040
  (1 shorter events, 0.0 us)
Async XLA Ops:
  7.2 243.5 %all-gather.2.cloned.1.call-start = ((), (), s32[]{:S(2)}) async-start(), calls=%async_computation.1 | async-start | bytes 23592960 | tf_op jit(solution)/shard_map/all_gather | solution.py:32
Sparse Core Ops, SparseCore 0:
  65.5 185.1 all-gather.1
